TPU v7x, 128 devices: a whole 4x4x4 slice. The times are simulated.
128 devices in a mesh: row: 16 (over z_lo, y, core), col: 8 (over x, z_hi).
Axes of the slice: x: 4, y: 4, z: 4 (z_hi: 2, z_lo: 2; z = z_hi * 2 + z_lo), core: 2. Of those that a mesh axis runs over, the one named last changes fastest.
Arguments:
- features: bfloat16 [262144, 256], P(('row', 'col')), may hold values from -6 to 6
- tiles: bfloat16 [16, 8, 768, 128, 128], P('row', 'col'), as said below
- tile_rows: int32 [16, 8, 768], P('row', 'col'), may hold values from 0 to 127
- tile_cols: int32 [16, 8, 768], P('row', 'col'), may hold values from 0 to 255
- valid: int32 [16, 8, 768], P('row', 'col'), may hold values from 0 to 1, as said below
- weight: bfloat16 [256, 256], replicated, may hold values from -0.375 to 0.375
- bias: float32 [256], replicated, may hold values from -3 to 3
Outputs:
- hidden: bfloat16 [262144, 256], P(('row', 'col'))
Inputs may be any that keep to these rules, and one draw needn't show every extreme that they name: Each cell holds between 96 and 384 valid slots at any positions; in every draw some cell has exactly 384 valid slots. `tiles`: tile entries are non-negative.
All inputs are finite; a program needn't handle non-finite values.
Results may differ from a plain program's by a relative error of at most 0.0039.
Values may be sent and summed in bfloat16 or wider, within the bound.
A program may use at most 256 MiB of HBM per device.

v0:
```python
import jax
import jax.numpy as jnp
from jax import lax
from jax.sharding import PartitionSpec as P


def on_device(features, tiles, tile_rows, tile_cols, valid, weight, bias):
    sub_rows = features.shape[0]
    width = features.shape[1]
    tile_size = tiles.shape[3]
    slot_count = tiles.shape[2]
    block_size = min(slot_count, 128)
    col_count = lax.axis_size("col")
    row_tiles = sub_rows * col_count // tile_size
    panel = lax.all_gather(features, "row", axis=0, tiled=True)
    panel_tiles = panel.reshape(-1, tile_size, width)
    cell_tiles = tiles[0, 0]
    cell_rows = tile_rows[0, 0]
    cell_cols = tile_cols[0, 0]
    cell_valid = valid[0, 0]
    start_sum = jnp.zeros((row_tiles, tile_size, width), jnp.float32)

    def add_block(partial_sum, tile_block, row_block, col_block, flag_block):
        chosen = panel_tiles[col_block]
        products = jnp.einsum(
            "bij,bjf->bif", tile_block, chosen, preferred_element_type=jnp.float32
        )
        products = products * flag_block.astype(jnp.float32)[:, None, None]
        return partial_sum.at[row_block].add(products)

    ordering = jnp.argsort(1 - cell_valid, stable=True)
    live_count = jnp.sum(cell_valid)
    turns = (live_count + block_size - 1) // block_size

    def loop_step(turn, partial_sum):
        picked = lax.dynamic_slice_in_dim(ordering, turn * block_size, block_size)
        return add_block(
            partial_sum,
            cell_tiles[picked],
            cell_rows[picked],
            cell_cols[picked],
            cell_valid[picked],
        )

    partial_sum = lax.fori_loop(0, turns, loop_step, start_sum)
    partial_rows = partial_sum.reshape(row_tiles * tile_size, width)
    summed = lax.psum_scatter(partial_rows, "col", scatter_dimension=0, tiled=True)
    aggregated = summed.astype(jnp.bfloat16)
    mixed = jnp.dot(aggregated, weight, preferred_element_type=jnp.float32) + bias
    return jnp.maximum(mixed, 0.0).astype(jnp.bfloat16)


def solution(mesh):
    return jax.shard_map(
        on_device,
        mesh=mesh,
        in_specs=(
            P(("row", "col"), None),
            P("row", "col", None, None, None),
            P("row", "col", None),
            P("row", "col", None),
            P("row", "col", None),
            P(),
            P(),
        ),
        out_specs=P(("row", "col"), None),
        check_vma=False,
    )
```

profile of v0, /device:TPU:1, one launch (start us, length us, event | category | flops | bytes accessed | tf_op | source)
XLA Modules:
  0.0 547.5 jit_solution(16613632500860429203)
XLA Ops:
  6.5 0.0 copy-start
  6.5 0.0 all-gather.2.cloned.1.call-start
  6.5 0.7 all-gather.2.cloned.1.call-update
  7.3 0.0 reduce-scatter.2.cloned.1.call-start
  7.3 1.3 fusion.5
  9.3 0.7 reduce.2
  10.0 0.7 reduce.3
  10.7 4.4 sort.17
  15.1 89.2 %all-gather.2.cloned.1.call-done = bf16[32768,256]{1,0:T(8,128)(2,1)} async-done(((bf16[2048,256]{1,0:T(8,128)(2,1)}), bf16[32768,256]{1,0:T(8,128)(2,1)}) %all-gather.2.cloned.1.call-update) | async-done | bytes 16777232 | tf_op jit(solution)/shard_map/all_gather | solution.py:15
  104.3 7.8 %broadcast_in_dim.4 = f32[128,128,256]{2,1,0:T(8,128)} broadcast(f32[]{:T(128)} %constant.32.clone.1), dimensions={} | broadcast | bytes 16777220 | tf_op jit(solution)/shard_map/broadcast_in_dim | solution.py:21
  112.1 77.9 %while.10 = (s32[]{:T(128)}, f32[128,128,256]{2,1,0:T(8,128)}, s32[]{:T(128)}, s32[768]{0:T(1024)S(1)}, s32[768]{0:T(1024)S(1)}, /*index=5*/bf16[768,128,128]{2,...) while((s32[]{:T(128)}, f32[128,128,256]{2,1,0:T(8,128)}, ...), condition=%wide.region_4.5_spmd, body=%wide.region_2.4_spmd.sunk | while | flops 1082133760 | bytes 104877744 | solution.py:45
  112.1 0.1 compare_select_fusion.4
  112.2 1.0 gather_fusion.4
  113.2 1.0 gather_fusion.2
  114.2 1.0 gather_fusion
  115.2 11.2 %gather_fusion.1 = bf16[128,128,128]{2,1,0:T(8,128)(2,1)} fusion(bf16[768,128,128]{2,1,0:T(8,128)(2,1)} %get-tuple-element.163, s32[1024]{0:T(1024)S(1)} %pad_clamp_fusion.4), kind=kCustom, calls=%fused_computation.1.clone.1 | custom fusion | bytes 8389120 | tf_op jit(solution)/shard_map/while/body/gather | solution.py:39
  126.3 12.3 %gather_fusion.3 = bf16[128,128,256]{2,1,0:T(8,128)(2,1)} fusion(bf16[256,128,256]{2,1,0:T(8,128)(2,1)} %get-tuple-element.165, s32[1024]{0:T(1024)S(1)} %pad_clamp_fusion.5), kind=kCustom, calls=%fused_computation.3.clone.1 | custom fusion | bytes 16777728 | tf_op jit(solution)/shard_map/while/body/gather | solution.py:24
  138.6 12.7 %convolution_multiply_fusion.2 = f32[128,128,256]{2,1,0:T(8,128)} fusion(bf16[128,128,128]{2,1,0:T(8,128)(2,1)} %gather_fusion.1, bf16[128,128,256]{2,1,0:T(8,128)(2,1)} %gather_fusion.3, f32[128]{0:T(128)S(1)} %convert_element_type.19), kind=kOutput, calls=%fused_computation.6.clone.1 | convolution fusion | flops 1077936128 | bytes 29360640 | tf_op jit(solution)/shard_map/while/body/bij,bjf->bif/dot_general | solution.py:25
  151.4 38.7 %scatter_fusion = f32[128,128,256]{2,1,0:T(8,128)} fusion(f32[128,128,256]{2,1,0:T(8,128)} %get-tuple-element.146, s32[128]{0:T(128)S(1)} %fusion.15, f32[128,128,256]{2,1,0:T(8,128)} %convolution_multiply_fusion.2), kind=kCustom, calls=%fused_computation.5.clone.1 | custom fusion | flops 4194304 | bytes 50332160 | tf_op jit(solution)/shard_map/while/body/scatter-add | solution.py:29
  190.0 0.0 copy-start.1
  190.0 0.0 reduce-scatter.2.cloned.1.call-update
  190.0 347.6 %reduce-scatter.2.cloned.1.call-done = f32[2048,256]{1,0:T(8,128)} async-done(((f32[16384,256]{1,0:T(8,128)}), f32[2048,256]{1,0:T(8,128)}) %reduce-scatter.2.cloned.1.call-update) | async-done | bytes 2097168 | tf_op jit(solution)/shard_map/reduce_scatter | solution.py:47
  537.7 0.0 copy-done
  537.7 0.0 copy-done.1
  537.7 3.0 fusion.3
  (7 shorter events, 0.0 us)
Async XLA Ops:
  6.5 531.2 %copy-start = (bf16[256,256]{1,0:T(8,128)(2,1)S(1)}, bf16[256,256]{1,0:T(8,128)(2,1)}, u32[]{:S(2)}) copy-start(bf16[256,256]{1,0:T(8,128)(2,1)} %param.14) | copy-start | bytes 393220
  6.5 97.7 %all-gather.2.cloned.1.call-start = ((), (), s32[]{:S(2)}) async-start(), calls=%async_computation.1 | async-start | bytes 17825792 | tf_op jit(solution)/shard_map/all_gather | solution.py:15
  7.3 530.4 %reduce-scatter.2.cloned.1.call-start = ((), (), s32[]{:S(2)}) async-start(), calls=%async_computation.2 | async-start | bytes 18874368 | tf_op jit(solution)/shard_map/reduce_scatter | solution.py:47
  190.0 347.7 %copy-start.1 = (f32[256]{0:T(256)S(1)}, f32[256]{0:T(256)}, u32[]{:S(2)}) copy-start(f32[256]{0:T(256)} %param.15) | copy-start | bytes 3076
Sparse Core Ops, SparseCore 0:
  9.0 95.1 all-gather.1
  190.2 347.4 reduce-scatter.1
where the time goes:
time: 550 us; the launch traced here: 548 us
  waiting for transfers between devices  438 us (80%)
  other arithmetic  45.9 us (8%)
  local copies, waits for them, and re-layouts  34.2 us (6%)
  matrix products  15.7 us (3%)
  between operations  14.1 us (3%)
    reduce_scatter x1, waiting for transfers between devices, on_device(): lax.psum_scatter(partial_rows, 'col', scatter_dimension=0, tiled=True)  348 us
    all_gather x1, waiting for transfers between devices, on_device(): panel = lax.all_gather(features, 'row', axis=0, tiled=True)  89.2 us
    scatter-add x1, other arithmetic, add_block(): return partial_sum.at[row_block].add(products)  38.7 us
    dot_general x1, matrix products, add_block(): jnp.einsum('bij,bjf->bif', tile_block, chosen, preferred_element_type=jnp...  12.7 us
    gather x1, local copies, waits for them, and re-layouts, add_block(): chosen = panel_tiles[col_block]  12.3 us
    gather x1, local copies, waits for them, and re-layouts, loop_step(): cell_tiles[picked]  11.2 us
  transfers between devices with their start and end apart: 2, of which 2 were waited for; matrix products, arithmetic and copies ran while one was open for 1% of the time, Pallas kernels for 0%

commit v1 on v0

v1 whole, which is shorter than its diff:
```python
import functools

import jax
import jax.numpy as jnp
from jax import lax
from jax.experimental import pallas as pl
from jax.experimental.pallas import tpu as pltpu
from jax.sharding import PartitionSpec as P

MESH = pl.DeviceIdType.MESH
Y, ZL, CORE, X, ZH = 4, 2, 2, 4, 2
UNROLL = 8
FORWARD = ((0, 0, 0), (0, 0, 1), (0, 1, 1), (-1, 0, 0), (-1, 1, 1))
BACKWARD = ((0, 0, 1), (0, 0, 0), (0, 1, 0), (1, 0, 1), (1, 1, 0))
ACROSS = ((0, 0, 1), (0, 0, 0), (-1, 0, 0), (1, 0, 1))
LANDED = (
    tuple((dy - 1, dz, up) for dy, dz, up in FORWARD)
    + tuple((dy + 1, dz, up) for dy, dz, up in BACKWARD)
    + tuple((dy, 1 - dz, up) for dy, dz, up in ACROSS)
)


def tables(rows, cols, valid, row_tiles, pairs):
    slots = rows.shape[0]
    ids = jnp.arange(slots, dtype=jnp.int32)
    key = jnp.where(valid > 0, rows, row_tiles)
    earlier = (key[:, None] == key[None, :]) & (ids[None, :] < ids[:, None])
    rank = jnp.sum(earlier.astype(jnp.int32), axis=1)
    row_ids = jnp.arange(row_tiles, dtype=jnp.int32)
    in_row = row_ids[:, None] == key[None, :]
    count = jnp.sum(in_row.astype(jnp.int32), axis=1)
    used = (count + 1) >> 1
    start = jnp.sum(jnp.where(row_ids[None, :] < row_ids[:, None], used[None, :], 0), axis=1)
    place = jnp.sum(jnp.where(in_row, 2 * start[:, None], 0), axis=0) + rank
    place = jnp.where(valid > 0, place, -1)
    at = place[None, :] == jnp.arange(2 * pairs, dtype=jnp.int32)[:, None]
    slot = jnp.sum(jnp.where(at, ids[None, :] - slots, 0), axis=1) + slots
    col = jnp.sum(jnp.where(at, cols[None, :], 0), axis=1)
    pair_ids = jnp.arange(pairs, dtype=jnp.int32)
    first = jnp.any((start[None, :] == pair_ids[:, None]) & (count > 0)[None, :], axis=1)
    keep = jnp.where(first, 0.0, 1.0).astype(jnp.float32)
    last = jnp.where(count > 0, start + used - 1, pairs)
    return slot, col, keep, last


def kernel(
    slots, pairs, row_tiles, block,
    slot, col, keep, last, features, tiles, weight, bias, out,
    tile_store, panel_a, panel_b, sums, part_a, got_a, got_b, agg_a, agg_b,
    own_sem, tile_sem, ring_send, ring_recv, twin_send, twin_recv, sum_send, sum_recv,
):
    half = block // 2
    row, column = lax.axis_index("row"), lax.axis_index("col")
    zl, y, core = row // (Y * CORE), (row // CORE) % Y, row % CORE
    x, zh = column // ZH, column % ZH

    def at_row(dy, dz, dc=0):
        return ((zl + dz) % ZL) * (Y * CORE) + ((y + dy + Y) % Y) * CORE + (core + dc) % CORE

    def at_column(dx, dz):
        return ((x + dx + X) % X) * ZH + (zh + dz) % ZH

    up_y, down_y = (at_row(1, 0), column), (at_row(-1, 0), column)
    other_z, twin = (at_row(0, 1), column), (at_row(0, 0, 1), column)
    up_x, down_x = (row, at_column(1, 0)), (row, at_column(-1, 0))
    far_z = (row, at_column(0, 1))

    panels, gots, aggs = (panel_a, panel_b), (got_a, got_b), (agg_a, agg_b)
    parts = (part_a, panel_a)

    def load_own(h):
        return pltpu.make_async_copy(
            features.at[:, :, pl.ds(h * 128, 128)],
            panels[h].at[pl.ds(row * block, block)],
            own_sem.at[h],
        )

    load_own(0).start()
    load_own(1).start()
    group = slots // tile_sem.shape[0]
    tile_loads = [
        pltpu.make_async_copy(
            tiles.at[pl.ds(i * group, group)], tile_store.at[pl.ds(i * group, group)], tile_sem.at[i]
        )
        for i in range(tile_sem.shape[0])
    ]
    barrier = pltpu.get_barrier_semaphore()
    peers = (up_y, down_y, other_z, twin, up_x, down_x, far_z)
    for peer in peers:
        pl.semaphore_signal(barrier, inc=1, device_id=peer, device_id_type=MESH)
    pl.semaphore_wait(barrier, len(peers))

    def piece(h, spot):
        dy, dz, up = spot
        return panels[h].at[pl.ds(at_row(dy, dz) * block + up * half, half)]

    def ring_copies(h):
        copies = []
        for target, spots in ((up_y, FORWARD), (down_y, BACKWARD), (other_z, ACROSS)):
            for spot in spots:
                k = len(copies)
                copies.append(
                    pltpu.make_async_remote_copy(
                        piece(h, spot), piece(h, spot), ring_send.at[h, k], ring_recv.at[h, k],
                        device_id=target, device_id_type=MESH,
                    )
                )
        return copies

    def twin_copies(h):
        return [
            pltpu.make_async_remote_copy(
                piece(h, spot), piece(h, spot), twin_send.at[h, k], twin_recv.at[h, k],
                device_id=twin, device_id_type=MESH,
            )
            for k, spot in enumerate(LANDED + ((0, 0, 0), (0, 0, 1)))
        ]

    ring = (ring_copies(0), ring_copies(1))
    sibling = (twin_copies(0), twin_copies(1))

    def gather_start(h):
        load_own(h).wait()
        for k in (0, 5, 10, 1, 6, 11):
            ring[h][k].start()
        sibling[h][14].start()
        sibling[h][15].start()

    def gather_step(h, k, then=()):
        ring[h][k].wait_recv()
        for k_next in then:
            ring[h][k_next].start()
        sibling[h][k].start()

    def gather_first(h):
        gather_step(h, 10, (2,))
        gather_step(h, 0, (3, 12))
        gather_step(h, 5, (8, 13))
        gather_step(h, 11, (7,))
        gather_step(h, 1)
        gather_step(h, 6)

    def gather_second(h):
        gather_step(h, 2, (4,))
        gather_step(h, 7, (9,))

    def gather_rest(h):
        for k in (12, 13, 3, 8, 4, 9):
            gather_step(h, k)
        for copy in sibling[h]:
            copy.wait_recv()

    def products(h, low, high, total):
        panel = panels[h]

        def body(i, total):
            for j in range(UNROLL):
                s = i * UNROLL + j
                left = jnp.concatenate([tile_store[slot[2 * s]], tile_store[slot[2 * s + 1]]], axis=1)
                right = jnp.concatenate([panel[col[2 * s]], panel[col[2 * s + 1]]], axis=0)
                total = total * keep[s] + jnp.dot(left, right, preferred_element_type=jnp.float32)
                sums[s] = total.astype(jnp.bfloat16)
            return total

        return lax.fori_loop(low // UNROLL, high // UNROLL, body, total)

    def collect(h):
        part = parts[h]

        def body(i, carry):
            for j in range(8):
                r = i * 8 + j
                part[r] = sums[last[r]]
            return carry

        lax.fori_loop(0, row_tiles // 8, body, 0)

    def spot(dx, dz, up):
        return pl.ds(at_column(dx, dz) * block + up * half, half)

    def sum_copies(h):
        copies = []
        for dz in (1, 0):
            for target, spots in (
                (up_x, ((2, dz, 0), (1, dz, 1), (1, dz, 0))),
                (down_x, ((2, dz, 1), (-1, dz, 0), (-1, dz, 1))),
            ):
                copies += [(target, s) for s in spots]
        copies += [(far_z, (0, 1, 0)), (far_z, (0, 1, 1))]
        return [
            pltpu.make_async_remote_copy(
                parts[h].at[spot(*s)], gots[h].at[k], sum_send.at[h, k], sum_recv.at[h, k],
                device_id=target, device_id_type=MESH,
            )
            for k, (target, s) in enumerate(copies)
        ]

    adds = (sum_copies(0), sum_copies(1))

    def wide(value):
        return value.astype(jnp.float32)

    def sum_start(h, i):
        for k in (0, 3, 1, 4):
            adds[h][6 * i + k].start()

    def sum_pass(h, i):
        part, got, dz = parts[h], gots[h], 1 - i
        for k, dx, up, k_next in ((0, 1, 0, 2), (3, -1, 1, 5)):
            adds[h][6 * i + k].wait_recv()
            here = spot(dx, dz, up)
            part[here] = (wide(part[here]) + wide(got[6 * i + k])).astype(jnp.bfloat16)
            adds[h][6 * i + k_next].start()

    def sum_across(h):
        part, got = parts[h], gots[h]
        for up, ks in ((0, (2, 4)), (1, (1, 5))):
            for k in ks:
                adds[h][k].wait_recv()
            here = spot(0, 1, up)
            part[here] = (wide(part[here]) + wide(got[ks[0]]) + wide(got[ks[1]])).astype(jnp.bfloat16)
            adds[h][12 + up].start()

    def sum_end(h):
        part, got, agg = parts[h], gots[h], aggs[h]
        for up, ks in ((1, (7, 11, 13)), (0, (8, 10, 12))):
            for k in ks:
                adds[h][k].wait_recv()
            total = wide(part[spot(0, 0, up)])
            for k in ks:
                total = total + wide(got[k])
            agg[pl.ds(up * half, half)] = total.astype(jnp.bfloat16)

    zero = jnp.zeros((128, 128), jnp.float32)
    gather_start(0)
    for copy in tile_loads:
        copy.start()
    tile_store[slots] = zero.astype(jnp.bfloat16)
    sums[pairs] = zero.astype(jnp.bfloat16)
    gather_first(0)
    gather_second(0)
    gather_start(1)
    gather_rest(0)
    for copy in tile_loads:
        copy.wait()
    products(0, 0, pairs, zero)
    collect(0)
    sum_start(0, 0)
    gather_first(1)
    sum_pass(0, 0)
    sum_start(0, 1)
    gather_second(1)
    gather_rest(1)
    sum_across(0)
    for copy in ring[0] + sibling[0]:
        copy.wait_send()
    total = products(1, 0, pairs // 2, zero)
    sum_pass(0, 1)
    products(1, pairs // 2, pairs, total)
    collect(1)
    sum_start(1, 0)
    sum_end(0)
    sum_pass(1, 0)
    sum_start(1, 1)
    sum_across(1)
    sum_pass(1, 1)
    sum_end(1)

    def finish(t, carry):
        mixed = jnp.dot(
            jnp.concatenate([agg_a[t], agg_b[t]], axis=1), weight[...], preferred_element_type=jnp.float32
        )
        out[t] = jnp.maximum(mixed + bias[...], 0.0).astype(jnp.bfloat16)
        return carry

    lax.fori_loop(0, block, finish, 0)
    for copy in ring[1] + sibling[1] + adds[0] + adds[1]:
        copy.wait_send()


def on_device(features, tiles, tile_rows, tile_cols, valid, weight, bias):
    sub_rows, width = features.shape
    size, slots = tiles.shape[3], tiles.shape[2]
    block = sub_rows // size
    row_tiles = block * X * ZH
    panel_tiles = block * Y * ZL * CORE
    pairs = (slots // 2 + row_tiles) // 2
    slot, col, keep, last = tables(tile_rows[0, 0], tile_cols[0, 0], valid[0, 0], row_tiles, pairs)
    smem, vmem = pl.BlockSpec(memory_space=pltpu.SMEM), pl.BlockSpec(memory_space=pltpu.VMEM)
    hbm = pl.BlockSpec(memory_space=pl.ANY)
    dma = pltpu.SemaphoreType.DMA

    def store(*shape):
        return pltpu.VMEM(shape + (size, size), jnp.bfloat16)

    hidden = pl.pallas_call(
        functools.partial(kernel, slots, pairs, row_tiles, block),
        name="graph_layer",
        out_shape=jax.ShapeDtypeStruct((block, size, width), jnp.bfloat16),
        in_specs=[smem, smem, smem, smem, hbm, hbm, vmem, vmem],
        out_specs=vmem,
        scratch_shapes=[
            store(slots + 1), store(panel_tiles), store(panel_tiles), store(pairs + 1), store(row_tiles),
            store(14, block // 2), store(14, block // 2), store(block), store(block),
            dma((2,)), dma((8,)), dma((2, 14)), dma((2, 14)), dma((2, 16)), dma((2, 16)), dma((2, 14)), dma((2, 14)),
        ],
        compiler_params=pltpu.CompilerParams(
            collective_id=0, has_side_effects=True, vmem_limit_bytes=67043328
        ),
    )(
        slot, col, keep, last,
        features.reshape(block, size, width), tiles.reshape(slots, size, size), weight, bias.reshape(1, width),
    )
    return hidden.reshape(sub_rows, width)


def solution(mesh):
    return jax.shard_map(
        on_device,
        mesh=mesh,
        in_specs=(
            P(("row", "col"), None),
            P("row", "col", None, None, None),
            P("row", "col", None),
            P("row", "col", None),
            P("row", "col", None),
            P(),
            P(),
        ),
        out_specs=P(("row", "col"), None),
        check_vma=False,
    )
```

time: 550 us -> 134 us (0.24)
  waiting for transfers between devices: 438 us -> 0 us
  Pallas kernels: 0 us -> 126 us
  other arithmetic: 45.9 us -> 5.71 us
  local copies, waits for them, and re-layouts: 34.2 us -> 2.26 us
  matrix products: 15.7 us -> 0 us
  between operations: 14.1 us -> 0.05 us
    reduce_scatter x1 -> x0, waiting for transfers between devices: 348 us -> none  [on_device(): lax.psum_scatter(partial_rows, 'col', scatter_dimension=0, tiled=True)]
    pallas_call x0 -> x1, Pallas kernels: none -> 126 us  [on_device(): pl.pallas_call(functools.partial(kernel, slots, pairs, row_tiles, block),...]
    all_gather x1 -> x0, waiting for transfers between devices: 89.2 us -> none  [on_device(): panel = lax.all_gather(features, 'row', axis=0, tiled=True)]
    scatter-add x1 -> x0, other arithmetic: 38.7 us -> none  [add_block(): return partial_sum.at[row_block].add(products)]
    gather x5 -> x0, local copies, waits for them, and re-layouts: 26.4 us -> none  [the longest x1 12.3 us: add_block(): chosen = panel_tiles[col_block]]
    dot_general x2 -> x0, matrix products: 15.7 us -> none  [the longest x1 12.7 us: add_block(): jnp.einsum('bij,bjf->bif', tile_block, chosen, preferred_element_type=jnp...]
    broadcast_in_dim x1 -> x0, local copies, waits for them, and re-layouts: 7.8 us -> none  [on_device(): start_sum = jnp.zeros((row_tiles, tile_size, width), jnp.float32)]
  transfers between devices with their start and end apart: 2 -> 0, of which waited for: 2 -> 0; matrix products, arithmetic and copies ran while one was open for 1% -> 0% of each run, Pallas kernels for 0% -> 0%
where the time goes in v1:
time: 134 us
  Pallas kernels  126 us (94%)
  other arithmetic  5.71 us (4%)
  local copies, waits for them, and re-layouts  2.26 us (2%)
    pallas_call x1, Pallas kernels, on_device(): pl.pallas_call(functools.partial(kernel, slots, pairs, row_tiles, block),...  126 us

profile of v1, /device:TPU:1, one launch (start us, length us, event | category | flops | bytes accessed | tf_op | source)
XLA Modules:
  0.0 133.9 jit_solution(10323641315423973398)
XLA Ops:
  0.0 0.7 compare_reduce_fusion
  0.7 0.7 reduce.1
  1.4 0.1 convert_reduce_fusion.1
  1.6 0.1 select_reduce_fusion.3
  1.7 0.1 fusion.2
  1.8 0.5 add_select_fusion.1
  2.3 0.6 broadcast_select_fusion.1.keep
  2.9 0.1 select_reduce_fusion.2
  3.1 0.4 convert_reduce_fusion
  3.4 0.7 reduce.2
  4.1 1.0 select_reduce_fusion
  5.2 0.6 broadcast_add_fusion.slot
  5.8 125.9 %graph_layer.1 = bf16[16,128,256]{2,1,0:T(8,128)(2,1)} custom-call(s32[512]{0:T(512)} %broadcast_add_fusion.slot, s32[512]{0:T(512)} %get-tuple-element.5.col, f32[256]{0:T(256)} %broadcast_select_fusion.1.keep, s32[128]{0:T(128)} %get-tuple-element.7.last, bf16[16,128,256]{2,1,0:T(8,128)(2,1)} %bitcast.6, bf16[768,128,128]{2,1,0:T(8,128)(2,1)} %bitcast.4, ...), custom_call_target="tpu_custom_call" | custom-call | tf_op jit(solution)/shard_map/graph_layer/pallas_call | solution.py:296
  131.6 2.3 %copy.9 = bf16[2048,256]{1,0:T(8,128)(2,1)} copy(bf16[2048,256]{1,0:T(8,128)(2,1)} %bitcast.5) | data formatting | bytes 2097152
  (4 shorter events, 0.0 us)

commit v2 on v1

v2 whole, which is shorter than its diff:
```python
import functools

import jax
import jax.numpy as jnp
from jax import lax
from jax.experimental import pallas as pl
from jax.experimental.pallas import tpu as pltpu
from jax.sharding import PartitionSpec as P

MESH = pl.DeviceIdType.MESH
Y, ZL, CORE, X, ZH = 4, 2, 2, 4, 2
CHUNKS = 4
UNROLL = 16
FORWARD = ((0, 0, 0), (0, 0, 1), (0, 1, 1), (-1, 0, 0), (-1, 1, 1))
BACKWARD = ((0, 0, 1), (0, 0, 0), (0, 1, 0), (1, 0, 1), (1, 1, 0))
ACROSS = ((0, 0, 1), (0, 0, 0), (-1, 0, 0), (1, 0, 1))
LANDED = (
    tuple((dy - 1, dz, up) for dy, dz, up in FORWARD)
    + tuple((dy + 1, dz, up) for dy, dz, up in BACKWARD)
    + tuple((dy, 1 - dz, up) for dy, dz, up in ACROSS)
)


def tables(rows, cols, valid, row_tiles, pairs, block):
    slots = rows.shape[0]
    ids = jnp.arange(slots, dtype=jnp.int32)
    key = jnp.where(valid > 0, rows, row_tiles)
    earlier = (key[:, None] == key[None, :]) & (ids[None, :] < ids[:, None])
    rank = jnp.sum(earlier.astype(jnp.int32), axis=1)
    row_ids = jnp.arange(row_tiles, dtype=jnp.int32)
    in_row = row_ids[:, None] == key[None, :]
    count = jnp.sum(in_row.astype(jnp.int32), axis=1)
    used = (count + 1) >> 1
    start = jnp.sum(jnp.where(row_ids[None, :] < row_ids[:, None], used[None, :], 0), axis=1)
    place = jnp.sum(jnp.where(in_row, 2 * start[:, None], 0), axis=0) + rank
    place = jnp.where(valid > 0, place, -1)
    at = place[None, :] == jnp.arange(2 * pairs, dtype=jnp.int32)[:, None]
    slot = jnp.sum(jnp.where(at, ids[None, :] - slots, 0), axis=1) + slots
    col = jnp.sum(jnp.where(at, cols[None, :], 0), axis=1)
    pair_ids = jnp.arange(pairs, dtype=jnp.int32)
    first = jnp.any((start[None, :] == pair_ids[:, None]) & (count > 0)[None, :], axis=1)
    keep = jnp.where(first, 0.0, 1.0).astype(jnp.float32)
    last = jnp.where(count > 0, start + used - 1, pairs)
    packed = (col // block) * (block // 2) + col % (block // 2)
    side = (col % block) // (block // 2)
    return slot, packed, side, keep, last


def kernel(
    slots, pairs, row_tiles, block,
    slot, col, side, keep, last, features, tiles, out,
    tile_store, panel_0, panel_1, panel_2, panel_3, sums, part_a, got_0, got_1, got_2, got_3, agg, sides,
    own_sem, tile_sem, ring_send, ring_recv, twin_send, twin_recv, sum_send, sum_recv,
):
    packs = block // 2
    half = packs // 2
    row, column = lax.axis_index("row"), lax.axis_index("col")
    zl, y, core = row // (Y * CORE), (row // CORE) % Y, row % CORE
    x, zh = column // ZH, column % ZH

    def at_row(dy, dz, dc=0):
        return ((zl + dz) % ZL) * (Y * CORE) + ((y + dy + Y) % Y) * CORE + (core + dc) % CORE

    def at_column(dx, dz):
        return ((x + dx + X) % X) * ZH + (zh + dz) % ZH

    up_y, down_y = (at_row(1, 0), column), (at_row(-1, 0), column)
    other_z, twin = (at_row(0, 1), column), (at_row(0, 0, 1), column)
    up_x, down_x = (row, at_column(1, 0)), (row, at_column(-1, 0))
    far_z = (row, at_column(0, 1))

    panels, gots = (panel_0, panel_1, panel_2, panel_3), (got_0, got_1, got_2, got_3)
    parts = ((part_a, 0), (part_a, row_tiles // 2), (panel_0, 0), (panel_1, 0))

    own = pltpu.make_async_copy(features, out, own_sem)
    own.start()
    barrier = pltpu.get_barrier_semaphore()
    peers = (up_y, down_y, other_z, twin, up_x, down_x, far_z)
    for peer in peers:
        pl.semaphore_signal(barrier, inc=1, device_id=peer, device_id_type=MESH)
    own.wait()

    def pack(h):
        for t in range(packs):
            low, high = out[t, :, pl.ds(128 * h, 128)], out[t + packs, :, pl.ds(128 * h, 128)]
            for c in (0, 1):
                lanes = slice(64 * c, 64 * c + 64)
                panels[2 * h + c][row * packs + t] = jnp.concatenate([low[:, lanes], high[:, lanes]], axis=1)

    pack(0)
    pl.semaphore_wait(barrier, len(peers))

    def piece(h, spot):
        dy, dz, up = spot
        return panels[h].at[pl.ds(at_row(dy, dz) * packs + up * half, half)]

    def ring_copies(h):
        copies = []
        for target, spots in ((up_y, FORWARD), (down_y, BACKWARD), (other_z, ACROSS)):
            for spot in spots:
                k = len(copies)
                copies.append(
                    pltpu.make_async_remote_copy(
                        piece(h, spot), piece(h, spot), ring_send.at[h, k], ring_recv.at[h, k],
                        device_id=target, device_id_type=MESH,
                    )
                )
        return copies

    def twin_copies(h):
        return [
            pltpu.make_async_remote_copy(
                piece(h, spot), piece(h, spot), twin_send.at[h, k], twin_recv.at[h, k],
                device_id=twin, device_id_type=MESH,
            )
            for k, spot in enumerate(LANDED + ((0, 0, 0), (0, 0, 1)))
        ]

    ring = [ring_copies(h) for h in range(CHUNKS)]
    sibling = [twin_copies(h) for h in range(CHUNKS)]

    def gather_start(h):
        for k in (0, 5, 10, 1, 6, 11):
            ring[h][k].start()
        sibling[h][14].start()
        sibling[h][15].start()

    def gather_step(h, k, then=()):
        ring[h][k].wait_recv()
        for k_next in then:
            ring[h][k_next].start()
        sibling[h][k].start()

    def gather_first(h):
        gather_step(h, 10, (2,))
        gather_step(h, 0, (3, 12))
        gather_step(h, 5, (8, 13))

    def gather_more(h):
        gather_step(h, 11, (7,))
        gather_step(h, 1)
        gather_step(h, 6)

    def gather_second(h):
        following = ring[h + 1] if h + 1 < CHUNKS else None
        if following:
            following[10].start()
            following[11].start()
        gather_step(h, 2, (4,))
        if following:
            following[0].start()
            following[1].start()
        gather_step(h, 7, (9,))
        if following:
            following[5].start()
            following[6].start()
            sibling[h + 1][14].start()
            sibling[h + 1][15].start()

    def gather_rest(h):
        for k in (12, 13, 3, 8, 4, 9):
            gather_step(h, k)
        for copy in sibling[h]:
            copy.wait_recv()

    def products(h, low, high, total):
        panel = panels[h]

        def body(i, total):
            for j in range(UNROLL):
                s = i * UNROLL + j
                left = jnp.concatenate([tile_store[slot[2 * s]], tile_store[slot[2 * s + 1]]], axis=1)
                right = jnp.concatenate(
                    [panel[col[2 * s + e]] * sides[side[2 * s + e]] for e in (0, 1)], axis=0
                )
                total = total * keep[s] + jnp.dot(left, right, preferred_element_type=jnp.float32)
                sums[s] = (total + pltpu.roll(total, 64, 1)).astype(jnp.bfloat16)
            return total

        return lax.fori_loop(low // UNROLL, high // UNROLL, body, total)

    def collect(h):
        part, base = parts[h]

        def body(q, carry):
            for t in range(packs):
                r = q * block + t
                part[base + q * packs + t] = sums[last[r]] * sides[0] + sums[last[r + packs]] * sides[1]
            return carry

        lax.fori_loop(0, X * ZH, body, 0)

    def spot(h, dx, dz, up):
        return pl.ds(parts[h][1] + at_column(dx, dz) * packs + up * half, half)

    def sum_copies(h):
        copies = []
        for dz in (1, 0):
            for target, spots in (
                (up_x, ((2, dz, 0), (1, dz, 1), (1, dz, 0))),
                (down_x, ((2, dz, 1), (-1, dz, 0), (-1, dz, 1))),
            ):
                copies += [(target, s) for s in spots]
        copies += [(far_z, (0, 1, 0)), (far_z, (0, 1, 1))]
        return [
            pltpu.make_async_remote_copy(
                parts[h][0].at[spot(h, *s)], gots[h].at[k], sum_send.at[h, k], sum_recv.at[h, k],
                device_id=target, device_id_type=MESH,
            )
            for k, (target, s) in enumerate(copies)
        ]

    adds = [sum_copies(h) for h in range(CHUNKS)]

    def wide(value):
        return value.astype(jnp.float32)

    def sum_start(h, i):
        for k in (0, 3, 1, 4):
            adds[h][6 * i + k].start()

    def sum_pass(h, i):
        part, got, dz = parts[h][0], gots[h], 1 - i
        for k, dx, up, k_next in ((0, 1, 0, 2), (3, -1, 1, 5)):
            adds[h][6 * i + k].wait_recv()
            here = spot(h, dx, dz, up)
            part[here] = (wide(part[here]) + wide(got[6 * i + k])).astype(jnp.bfloat16)
            adds[h][6 * i + k_next].start()

    def sum_across(h):
        part, got = parts[h][0], gots[h]
        for up, ks in ((0, (2, 4)), (1, (1, 5))):
            for k in ks:
                adds[h][k].wait_recv()
            here = spot(h, 0, 1, up)
            part[here] = (wide(part[here]) + wide(got[ks[0]]) + wide(got[ks[1]])).astype(jnp.bfloat16)
            adds[h][12 + up].start()

    def sum_end(h):
        part, got = parts[h][0], gots[h]
        for up, ks in ((1, (7, 11, 13)), (0, (8, 10, 12))):
            for k in ks:
                adds[h][k].wait_recv()
            total = wide(part[spot(h, 0, 0, up)])
            for k in ks:
                total = total + wide(got[k])
            total = total.astype(jnp.bfloat16)
            if h % 2 == 0:
                agg[pl.ds(up * half, half)] = total
            else:
                lanes = pl.ds(128 * (h // 2), 128)
                for t in range(half):
                    before, now = agg[up * half + t], total[t]
                    out[up * half + t, :, lanes] = jnp.concatenate([before[:, :64], now[:, :64]], axis=1)
                    out[packs + up * half + t, :, lanes] = jnp.concatenate([before[:, 64:], now[:, 64:]], axis=1)

    gather_start(0)
    group = slots // tile_sem.shape[0]
    tile_loads = [
        pltpu.make_async_copy(
            tiles.at[pl.ds(i * group, group)], tile_store.at[pl.ds(i * group, group)], tile_sem.at[i]
        )
        for i in range(tile_sem.shape[0])
    ]
    for copy in tile_loads:
        copy.start()
    pack(1)
    zero = jnp.zeros((128, 128), jnp.float32)
    tile_store[slots] = zero.astype(jnp.bfloat16)
    sums[pairs] = zero.astype(jnp.bfloat16)
    lane = lax.broadcasted_iota(jnp.int32, (1, 128), 1)
    sides[0] = jnp.where(lane < 64, 1.0, 0.0).astype(jnp.bfloat16)
    sides[1] = jnp.where(lane < 64, 0.0, 1.0).astype(jnp.bfloat16)
    gather_first(0)
    gather_more(0)
    gather_second(0)
    quarter, end = pairs // 4, CHUNKS - 1
    for h in range(CHUNKS):
        gather_rest(h)
        if h == 0:
            for copy in tile_loads:
                copy.wait()
        if h > 0:
            sum_pass(h - 1, 0)
        total = products(h, 0, quarter, zero)
        if h < end:
            gather_first(h + 1)
        total = products(h, quarter, 2 * quarter, total)
        if h < end:
            gather_more(h + 1)
        total = products(h, 2 * quarter, 3 * quarter, total)
        if h > 0:
            sum_pass(h - 1, 1)
        products(h, 3 * quarter, pairs, total)
        if h > 1:
            for copy in ring[h - 2] + sibling[h - 2]:
                copy.wait_send()
        collect(h)
        sum_start(h, 0)
        if h < end:
            sum_start(h, 1)
            gather_second(h + 1)
        if h > 0:
            sum_across(h - 1)
        if h > 1:
            sum_end(h - 2)
    sum_pass(end, 0)
    sum_start(end, 1)
    sum_end(end - 1)
    sum_across(end)
    sum_pass(end, 1)
    sum_end(end)
    for copy in sum(ring[2:] + sibling[2:] + adds, []):
        copy.wait_send()


def on_device(features, tiles, tile_rows, tile_cols, valid, weight, bias):
    sub_rows, width = features.shape
    size, slots = tiles.shape[3], tiles.shape[2]
    block = sub_rows // size
    row_tiles = block * X * ZH
    packs = block // 2
    pairs = (slots // 2 + row_tiles) // 2
    slot, col, side, keep, last = tables(
        tile_rows[0, 0], tile_cols[0, 0], valid[0, 0], row_tiles, pairs, block
    )
    smem, vmem = pl.BlockSpec(memory_space=pltpu.SMEM), pl.BlockSpec(memory_space=pltpu.VMEM)
    hbm = pl.BlockSpec(memory_space=pl.ANY)
    dma = pltpu.SemaphoreType.DMA

    def store(*shape):
        return pltpu.VMEM(shape + (size, size), jnp.bfloat16)

    aggregated = pl.pallas_call(
        functools.partial(kernel, slots, pairs, row_tiles, block),
        name="graph_layer",
        out_shape=jax.ShapeDtypeStruct((block, size, width), jnp.bfloat16),
        in_specs=[smem, smem, smem, smem, smem, hbm, hbm],
        out_specs=vmem,
        scratch_shapes=[
            store(slots + 1),
            *[store(packs * Y * ZL * CORE)] * CHUNKS,
            store(pairs + 1),
            store(row_tiles),
            *[store(14, packs // 2)] * CHUNKS,
            store(packs),
            pltpu.VMEM((2, 1, size), jnp.bfloat16),
            dma, dma((8,)), *[dma((CHUNKS, 14))] * 2, *[dma((CHUNKS, 16))] * 2, *[dma((CHUNKS, 14))] * 2,
        ],
        compiler_params=pltpu.CompilerParams(
            collective_id=0, has_side_effects=True, vmem_limit_bytes=67043328
        ),
    )(
        slot, col, side, keep, last,
        features.reshape(block, size, width), tiles.reshape(slots, size, size),
    )
    mixed = jnp.dot(aggregated.reshape(sub_rows, width), weight, preferred_element_type=jnp.float32) + bias
    return jnp.maximum(mixed, 0.0).astype(jnp.bfloat16)


def solution(mesh):
    return jax.shard_map(
        on_device,
        mesh=mesh,
        in_specs=(
            P(("row", "col"), None),
            P("row", "col", None, None, None),
            P("row", "col", None),
            P("row", "col", None),
            P("row", "col", None),
            P(),
            P(),
        ),
        out_specs=P(("row", "col"), None),
        check_vma=False,
    )
```

time: 134 us -> 119 us (0.89)
  Pallas kernels: 126 us -> 111 us
  matrix products: 0 us -> 2.71 us
  local copies, waits for them, and re-layouts: 2.26 us -> 0 us
    pallas_call x1, Pallas kernels: 126 us -> 111 us  [on_device(): pl.pallas_call(functools.partial(kernel, slots, pairs, row_tiles, block),...]
    dot_general x0 -> x1, matrix products: none -> 2.71 us  [on_device(): jnp.dot(aggregated.reshape(sub_rows, width), weight, preferred_element_ty...]
    unnamed x1 -> x0, local copies, waits for them, and re-layouts: 2.26 us -> none
where the time goes in v2:
time: 119 us
  Pallas kernels  111 us (93%)
  other arithmetic  5.26 us (4%)
  matrix products  2.71 us (2%)
    pallas_call x1, Pallas kernels, on_device(): pl.pallas_call(functools.partial(kernel, slots, pairs, row_tiles, block),...  111 us
    dot_general x1, matrix products, on_device(): jnp.dot(aggregated.reshape(sub_rows, width), weight, preferred_element_ty...  2.71 us

profile of v2, /device:TPU:1, one launch (start us, length us, event | category | flops | bytes accessed | tf_op | source)
XLA Modules:
  0.0 118.9 jit_solution(16081367150108908215)
XLA Ops:
  0.0 0.7 compare_reduce_fusion
  0.7 0.7 reduce.1
  1.4 0.1 convert_reduce_fusion.1
  1.6 0.1 select_reduce_fusion.3
  1.7 0.1 fusion.4
  1.8 0.6 add_select_fusion.5
  2.4 0.6 broadcast_select_fusion.1.keep
  2.9 0.1 select_reduce_fusion.2
  3.1 0.4 convert_reduce_fusion
  3.4 0.7 reduce.2
  4.2 0.5 select_reduce_fusion
  4.7 0.6 add_select_fusion.1
  5.3 110.8 %graph_layer.1 = bf16[16,128,256]{2,1,0:T(8,128)(2,1)} custom-call(s32[512]{0:T(512)} %get-tuple-element.11.slot, s32[512]{0:T(512)} %get-tuple-element.8.col, s32[512]{0:T(512)} %get-tuple-element.7.side, f32[256]{0:T(256)} %broadcast_select_fusion.1.keep, s32[128]{0:T(128)} %get-tuple-element.9.last, bf16[16,128,256]{2,1,0:T(8,128)(2,1)} %bitcast.6, ...), custom_call_target="tpu_custom_call" | custom-call | tf_op jit(solution)/shard_map/graph_layer/pallas_call | solution.py:334
  116.2 2.7 %fusion.1 = bf16[2048,256]{1,0:T(8,128)(2,1)} fusion(bf16[2048,256]{1,0:T(8,128)(2,1)} %bitcast.7, bf16[256,256]{1,0:T(8,128)(2,1)} %param.12, f32[256]{0:T(256)} %param.13), kind=kOutput, calls=%fused_computation.2 | convolution fusion | flops 270008320 | bytes 2229248 | tf_op jit(solution)/shard_map/dot_general | solution.py:357
  (5 shorter events, 0.0 us)

commit v3 on v2

--- a/solution.py
+++ b/solution.py
@@ -21,39 +21,56 @@
 )
 
 
-def tables(rows, cols, valid, row_tiles, pairs, block):
-    slots = rows.shape[0]
-    ids = jnp.arange(slots, dtype=jnp.int32)
+def tables(rows, cols, valid, code_ref, keep_ref, last_ref, row_tiles, pairs, block):
+    slots, width, packs = rows.shape[1], row_tiles, block // 2
+    span = 2 * packs * Y * ZL * CORE
+
+    def iota(shape, axis):
+        return lax.broadcasted_iota(jnp.int32, shape, axis)
+
+    square = (width, width)
+    eye = iota(square, 0) == iota(square, 1)
+    row_ids = iota(square, 1)
+
+    def upright(line):
+        return jnp.sum(jnp.where(eye, line, 0), axis=1, keepdims=True)
+
     key = jnp.where(valid > 0, rows, row_tiles)
-    earlier = (key[:, None] == key[None, :]) & (ids[None, :] < ids[:, None])
-    rank = jnp.sum(earlier.astype(jnp.int32), axis=1)
-    row_ids = jnp.arange(row_tiles, dtype=jnp.int32)
-    in_row = row_ids[:, None] == key[None, :]
-    count = jnp.sum(in_row.astype(jnp.int32), axis=1)
+    place_in_panel = ((cols // block) * packs + cols % packs) * 2 + (cols % block) // packs
+    keys, codes, ranks = [], [], []
+    count = jnp.zeros((1, width), jnp.int32)
+    for b in range(slots // width):
+        lanes = slice(b * width, (b + 1) * width)
+        keys.append(upright(key[:, lanes]))
+        ids = b * width + iota((width, 1), 0)
+        codes.append((ids - slots) * span + upright(place_in_panel[:, lanes]))
+        earlier = (keys[b] == key) & (iota((width, slots), 1) < ids)
+        ranks.append(jnp.sum(earlier.astype(jnp.int32), axis=1, keepdims=True))
+        count += jnp.sum((keys[b] == row_ids).astype(jnp.int32), axis=0, keepdims=True)
     used = (count + 1) >> 1
-    start = jnp.sum(jnp.where(row_ids[None, :] < row_ids[:, None], used[None, :], 0), axis=1)
-    place = jnp.sum(jnp.where(in_row, 2 * start[:, None], 0), axis=0) + rank
-    place = jnp.where(valid > 0, place, -1)
-    at = place[None, :] == jnp.arange(2 * pairs, dtype=jnp.int32)[:, None]
-    slot = jnp.sum(jnp.where(at, ids[None, :] - slots, 0), axis=1) + slots
-    col = jnp.sum(jnp.where(at, cols[None, :], 0), axis=1)
-    pair_ids = jnp.arange(pairs, dtype=jnp.int32)
-    first = jnp.any((start[None, :] == pair_ids[:, None]) & (count > 0)[None, :], axis=1)
-    keep = jnp.where(first, 0.0, 1.0).astype(jnp.float32)
-    last = jnp.where(count > 0, start + used - 1, pairs)
-    packed = (col // block) * (block // 2) + col % (block // 2)
-    side = (col % block) // (block // 2)
-    return slot, packed, side, keep, last
+    start = jnp.sum(jnp.where(iota(square, 0) < row_ids, upright(used), 0), axis=0, keepdims=True)
+    code = jnp.full((1, 2 * pairs), slots * span, jnp.int32)
+    order = iota((width, 2 * pairs), 1)
+    for b in range(slots // width):
+        at = ranks[b] + 2 * jnp.sum(jnp.where(keys[b] == row_ids, start, 0), axis=1, keepdims=True)
+        at = jnp.where(keys[b] < row_tiles, at, -1)
+        code += jnp.sum(jnp.where(at == order, codes[b], 0), axis=0, keepdims=True)
+    code_ref[...] = code
+    first = upright(jnp.where(count > 0, start, -1)) == iota((width, pairs), 1)
+    keep_ref[...] = 1.0 - jnp.sum(first.astype(jnp.float32), axis=0, keepdims=True)
+    last_ref[...] = jnp.where(count > 0, start + used - 1, pairs)
 
 
 def kernel(
     slots, pairs, row_tiles, block,
-    slot, col, side, keep, last, features, tiles, out,
+    rows, cols, valid, features, tiles, out,
     tile_store, panel_0, panel_1, panel_2, panel_3, sums, part_a, got_0, got_1, got_2, got_3, agg, sides,
-    own_sem, tile_sem, ring_send, ring_recv, twin_send, twin_recv, sum_send, sum_recv,
+    code_line, keep_line, last_line, code, keep, last, table_sem, own_sem, tile_sem, ring_send, ring_recv, twin_send, twin_recv, sum_send, sum_recv,
 ):
     packs = block // 2
     half = packs // 2
+    span = 2 * packs * Y * ZL * CORE
+    shift = span.bit_length() - 1
     row, column = lax.axis_index("row"), lax.axis_index("col")
     zl, y, core = row // (Y * CORE), (row // CORE) % Y, row % CORE
     x, zh = column // ZH, column % ZH
@@ -169,11 +186,10 @@
         def body(i, total):
             for j in range(UNROLL):
                 s = i * UNROLL + j
-                left = jnp.concatenate([tile_store[slot[2 * s]], tile_store[slot[2 * s + 1]]], axis=1)
-                right = jnp.concatenate(
-                    [panel[col[2 * s + e]] * sides[side[2 * s + e]] for e in (0, 1)], axis=0
-                )
-                total = total * keep[s] + jnp.dot(left, right, preferred_element_type=jnp.float32)
+                pair = [code[0, 2 * s], code[0, 2 * s + 1]]
+                left = jnp.concatenate([tile_store[c >> shift] for c in pair], axis=1)
+                right = jnp.concatenate([panel[(c & (span - 1)) >> 1] * sides[c & 1] for c in pair], axis=0)
+                total = total * keep[0, s] + jnp.dot(left, right, preferred_element_type=jnp.float32)
                 sums[s] = (total + pltpu.roll(total, 64, 1)).astype(jnp.bfloat16)
             return total
 
@@ -185,7 +201,7 @@
         def body(q, carry):
             for t in range(packs):
                 r = q * block + t
-                part[base + q * packs + t] = sums[last[r]] * sides[0] + sums[last[r + packs]] * sides[1]
+                part[base + q * packs + t] = sums[last[0, r]] * sides[0] + sums[last[0, r + packs]] * sides[1]
             return carry
 
         lax.fori_loop(0, X * ZH, body, 0)
@@ -271,14 +287,21 @@
     lane = lax.broadcasted_iota(jnp.int32, (1, 128), 1)
     sides[0] = jnp.where(lane < 64, 1.0, 0.0).astype(jnp.bfloat16)
     sides[1] = jnp.where(lane < 64, 0.0, 1.0).astype(jnp.bfloat16)
+    tables(rows[...], cols[...], valid[...], code_line, keep_line, last_line, row_tiles, pairs, block)
+    table_loads = [
+        pltpu.make_async_copy(line, table, table_sem.at[i])
+        for i, (line, table) in enumerate(((code_line, code), (keep_line, keep), (last_line, last)))
+    ]
     gather_first(0)
+    for copy in table_loads:
+        copy.start()
     gather_more(0)
     gather_second(0)
     quarter, end = pairs // 4, CHUNKS - 1
     for h in range(CHUNKS):
         gather_rest(h)
         if h == 0:
-            for copy in tile_loads:
+            for copy in tile_loads + table_loads:
                 copy.wait()
         if h > 0:
             sum_pass(h - 1, 0)
@@ -321,11 +344,7 @@
     row_tiles = block * X * ZH
     packs = block // 2
     pairs = (slots // 2 + row_tiles) // 2
-    slot, col, side, keep, last = tables(
-        tile_rows[0, 0], tile_cols[0, 0], valid[0, 0], row_tiles, pairs, block
-    )
-    smem, vmem = pl.BlockSpec(memory_space=pltpu.SMEM), pl.BlockSpec(memory_space=pltpu.VMEM)
-    hbm = pl.BlockSpec(memory_space=pl.ANY)
+    vmem, hbm = pl.BlockSpec(memory_space=pltpu.VMEM), pl.BlockSpec(memory_space=pl.ANY)
     dma = pltpu.SemaphoreType.DMA
 
     def store(*shape):
@@ -335,7 +354,7 @@
         functools.partial(kernel, slots, pairs, row_tiles, block),
         name="graph_layer",
         out_shape=jax.ShapeDtypeStruct((block, size, width), jnp.bfloat16),
-        in_specs=[smem, smem, smem, smem, smem, hbm, hbm],
+        in_specs=[vmem, vmem, vmem, hbm, hbm],
         out_specs=vmem,
         scratch_shapes=[
             store(slots + 1),
@@ -345,13 +364,15 @@
             *[store(14, packs // 2)] * CHUNKS,
             store(packs),
             pltpu.VMEM((2, 1, size), jnp.bfloat16),
-            dma, dma((8,)), *[dma((CHUNKS, 14))] * 2, *[dma((CHUNKS, 16))] * 2, *[dma((CHUNKS, 14))] * 2,
+            pltpu.VMEM((1, 2 * pairs), jnp.int32), pltpu.VMEM((1, pairs), jnp.float32), pltpu.VMEM((1, row_tiles), jnp.int32),
+            pltpu.SMEM((1, 2 * pairs), jnp.int32), pltpu.SMEM((1, pairs), jnp.float32), pltpu.SMEM((1, row_tiles), jnp.int32),
+            dma((3,)), dma, dma((8,)), *[dma((CHUNKS, 14))] * 2, *[dma((CHUNKS, 16))] * 2, *[dma((CHUNKS, 14))] * 2,
         ],
         compiler_params=pltpu.CompilerParams(
             collective_id=0, has_side_effects=True, vmem_limit_bytes=67043328
         ),
     )(
-        slot, col, side, keep, last,
+        tile_rows[0], tile_cols[0], valid[0],
         features.reshape(block, size, width), tiles.reshape(slots, size, size),
     )
     mixed = jnp.dot(aggregated.reshape(sub_rows, width), weight, preferred_element_type=jnp.float32) + bias

time: 119 us -> 114 us (0.958)
  other arithmetic: 5.26 us -> 0 us
    select_n x5 -> x0, other arithmetic: 1.77 us -> none  [the longest x1 0.61 us: tables(): side = col % block // (block // 2)]
    unnamed x2 -> x0, other arithmetic: 1.4 us -> none
    reduce_sum x5 -> x0, other arithmetic: 1.24 us -> none  [the longest x1 0.54 us: tables(): col = jnp.sum(jnp.where(at, cols[None, :], 0), axis=1)]
where the time goes in v3:
time: 114 us
  Pallas kernels  111 us (97%)
  matrix products  2.72 us (2%)
    pallas_call x1, Pallas kernels, on_device(): pl.pallas_call(functools.partial(kernel, slots, pairs, row_tiles, block),...  111 us
    dot_general x1, matrix products, on_device(): jnp.dot(aggregated.reshape(sub_rows, width), weight, preferred_element_ty...  2.72 us

profile of v3, /device:TPU:1, one launch (start us, length us, event | category | flops | bytes accessed | tf_op | source)
XLA Modules:
  0.0 113.5 jit_solution(7043384185296331009)
XLA Ops:
  0.0 110.8 %graph_layer.1 = bf16[16,128,256]{2,1,0:T(8,128)(2,1)} custom-call(s32[1,768]{1,0:T(1,128)} %bitcast.11, s32[1,768]{1,0:T(1,128)} %bitcast.12, s32[1,768]{1,0:T(1,128)} %bitcast.13, bf16[16,128,256]{2,1,0:T(8,128)(2,1)} %bitcast.9, bf16[768,128,128]{2,1,0:T(8,128)(2,1)} %bitcast.8), custom_call_target="tpu_custom_call" | custom-call | tf_op jit(solution)/shard_map/graph_layer/pallas_call | solution.py:353
  110.8 2.7 %fusion.1 = bf16[2048,256]{1,0:T(8,128)(2,1)} fusion(bf16[2048,256]{1,0:T(8,128)(2,1)} %bitcast.10, bf16[256,256]{1,0:T(8,128)(2,1)} %param.12, f32[256]{0:T(256)} %param.13), kind=kOutput, calls=%fused_computation.2 | convolution fusion | flops 270008320 | bytes 2229248 | tf_op jit(solution)/shard_map/dot_general | solution.py:378

commit v4 on v3

--- a/solution.py
+++ b/solution.py
@@ -10,7 +10,7 @@
 MESH = pl.DeviceIdType.MESH
 Y, ZL, CORE, X, ZH = 4, 2, 2, 4, 2
 CHUNKS = 4
-UNROLL = 16
+UNROLL = 32
 FORWARD = ((0, 0, 0), (0, 0, 1), (0, 1, 1), (-1, 0, 0), (-1, 1, 1))
 BACKWARD = ((0, 0, 1), (0, 0, 0), (0, 1, 0), (1, 0, 1), (1, 1, 0))
 ACROSS = ((0, 0, 1), (0, 0, 0), (-1, 0, 0), (1, 0, 1))
@@ -118,7 +118,7 @@
                 k = len(copies)
                 copies.append(
                     pltpu.make_async_remote_copy(
-                        piece(h, spot), piece(h, spot), ring_send.at[h, k], ring_recv.at[h, k],
+                        piece(h, spot), piece(h, spot), ring_send.at[h], ring_recv.at[h, k],
                         device_id=target, device_id_type=MESH,
                     )
                 )
@@ -127,11 +127,19 @@
     def twin_copies(h):
         return [
             pltpu.make_async_remote_copy(
-                piece(h, spot), piece(h, spot), twin_send.at[h, k], twin_recv.at[h, k],
+                piece(h, spot), piece(h, spot), twin_send.at[h], twin_recv.at[h],
                 device_id=twin, device_id_type=MESH,
             )
             for k, spot in enumerate(LANDED + ((0, 0, 0), (0, 0, 1)))
         ]
+
+    def whole(pieces, send, recv):
+        ref = panel_2.at[pl.ds(0, pieces * half)]
+        return pltpu.make_async_remote_copy(ref, ref, send, recv, device_id=twin, device_id_type=MESH)
+
+    def gather_sent(h):
+        whole(14, ring_send.at[h], ring_recv.at[h, 0]).wait_send()
+        whole(16, twin_send.at[h], twin_recv.at[h]).wait_send()
 
     ring = [ring_copies(h) for h in range(CHUNKS)]
     sibling = [twin_copies(h) for h in range(CHUNKS)]
@@ -177,15 +185,14 @@
     def gather_rest(h):
         for k in (12, 13, 3, 8, 4, 9):
             gather_step(h, k)
-        for copy in sibling[h]:
-            copy.wait_recv()
+        whole(16, twin_send.at[h], twin_recv.at[h]).wait_recv()
 
     def products(h, low, high, total):
-        panel = panels[h]
+        panel, unroll = panels[h], UNROLL
 
         def body(i, total):
-            for j in range(UNROLL):
-                s = i * UNROLL + j
+            for j in range(unroll):
+                s = i * unroll + j
                 pair = [code[0, 2 * s], code[0, 2 * s + 1]]
                 left = jnp.concatenate([tile_store[c >> shift] for c in pair], axis=1)
                 right = jnp.concatenate([panel[(c & (span - 1)) >> 1] * sides[c & 1] for c in pair], axis=0)
@@ -193,18 +200,21 @@
                 sums[s] = (total + pltpu.roll(total, 64, 1)).astype(jnp.bfloat16)
             return total
 
-        return lax.fori_loop(low // UNROLL, high // UNROLL, body, total)
+        return lax.fori_loop(low // unroll, high // unroll, body, total)
 
     def collect(h):
         part, base = parts[h]
-
-        def body(q, carry):
+        order = ((2, 1), (1, 1), (-1, 1), (2, 0), (1, 0), (-1, 0), (0, 1), (0, 0))
+        ready = {0: (0, 3), 1: (1,), 2: (4,)}
+        if h < CHUNKS - 1:
+            ready |= {3: (6, 9), 4: (7,), 5: (10,)}
+        for i, (dx, dz) in enumerate(order):
+            q = at_column(dx, dz)
             for t in range(packs):
                 r = q * block + t
                 part[base + q * packs + t] = sums[last[0, r]] * sides[0] + sums[last[0, r + packs]] * sides[1]
-            return carry
-
-        lax.fori_loop(0, X * ZH, body, 0)
+            for k in ready.get(i, ()):
+                adds[h][k].start()
 
     def spot(h, dx, dz, up):
         return pl.ds(parts[h][1] + at_column(dx, dz) * packs + up * half, half)
@@ -220,7 +230,7 @@
         copies += [(far_z, (0, 1, 0)), (far_z, (0, 1, 1))]
         return [
             pltpu.make_async_remote_copy(
-                parts[h][0].at[spot(h, *s)], gots[h].at[k], sum_send.at[h, k], sum_recv.at[h, k],
+                parts[h][0].at[spot(h, *s)], gots[h].at[k], sum_send.at[h], sum_recv.at[h, k],
                 device_id=target, device_id_type=MESH,
             )
             for k, (target, s) in enumerate(copies)
@@ -316,12 +326,9 @@
             sum_pass(h - 1, 1)
         products(h, 3 * quarter, pairs, total)
         if h > 1:
-            for copy in ring[h - 2] + sibling[h - 2]:
-                copy.wait_send()
+            gather_sent(h - 2)
         collect(h)
-        sum_start(h, 0)
         if h < end:
-            sum_start(h, 1)
             gather_second(h + 1)
         if h > 0:
             sum_across(h - 1)
@@ -333,8 +340,10 @@
     sum_across(end)
     sum_pass(end, 1)
     sum_end(end)
-    for copy in sum(ring[2:] + sibling[2:] + adds, []):
-        copy.wait_send()
+    for h in range(CHUNKS):
+        if h > 1:
+            gather_sent(h)
+        whole(14, sum_send.at[h], sum_recv.at[h, 0]).wait_send()
 
 
 def on_device(features, tiles, tile_rows, tile_cols, valid, weight, bias):
@@ -366,7 +375,7 @@
             pltpu.VMEM((2, 1, size), jnp.bfloat16),
             pltpu.VMEM((1, 2 * pairs), jnp.int32), pltpu.VMEM((1, pairs), jnp.float32), pltpu.VMEM((1, row_tiles), jnp.int32),
             pltpu.SMEM((1, 2 * pairs), jnp.int32), pltpu.SMEM((1, pairs), jnp.float32), pltpu.SMEM((1, row_tiles), jnp.int32),
-            dma((3,)), dma, dma((8,)), *[dma((CHUNKS, 14))] * 2, *[dma((CHUNKS, 16))] * 2, *[dma((CHUNKS, 14))] * 2,
+            dma((3,)), dma, dma((8,)), dma((CHUNKS,)), dma((CHUNKS, 14)), dma((CHUNKS,)), dma((CHUNKS,)), dma((CHUNKS,)), dma((CHUNKS, 14)),
         ],
         compiler_params=pltpu.CompilerParams(
             collective_id=0, has_side_effects=True, vmem_limit_bytes=67043328

time: 114 us -> 109 us (0.956)
  Pallas kernels: 111 us -> 106 us
    pallas_call x1, Pallas kernels: 111 us -> 106 us  [on_device(): pl.pallas_call(functools.partial(kernel, slots, pairs, row_tiles, block),...]
where the time goes in v4:
time: 109 us
  Pallas kernels  106 us (97%)
  matrix products  2.72 us (2%)
    pallas_call x1, Pallas kernels, on_device(): pl.pallas_call(functools.partial(kernel, slots, pairs, row_tiles, block),...  106 us
    dot_general x1, matrix products, on_device(): jnp.dot(aggregated.reshape(sub_rows, width), weight, preferred_element_ty...  2.72 us

profile of v4, /device:TPU:1, one launch (start us, length us, event | category | flops | bytes accessed | tf_op | source)
XLA Modules:
  0.0 108.7 jit_solution(12165562247081162621)
XLA Ops:
  0.0 105.9 %graph_layer.1 = bf16[16,128,256]{2,1,0:T(8,128)(2,1)} custom-call(s32[1,768]{1,0:T(1,128)} %bitcast.11, s32[1,768]{1,0:T(1,128)} %bitcast.12, s32[1,768]{1,0:T(1,128)} %bitcast.13, bf16[16,128,256]{2,1,0:T(8,128)(2,1)} %bitcast.9, bf16[768,128,128]{2,1,0:T(8,128)(2,1)} %bitcast.8), custom_call_target="tpu_custom_call" | custom-call | tf_op jit(solution)/shard_map/graph_layer/pallas_call | solution.py:362
  106.0 2.7 %fusion.1 = bf16[2048,256]{1,0:T(8,128)(2,1)} fusion(bf16[2048,256]{1,0:T(8,128)(2,1)} %bitcast.10, bf16[256,256]{1,0:T(8,128)(2,1)} %param.12, f32[256]{0:T(256)} %param.13), kind=kOutput, calls=%fused_computation.2 | convolution fusion | flops 270008320 | bytes 2229248 | tf_op jit(solution)/shard_map/dot_general | solution.py:387

commit v5 on v4

--- a/solution.py
+++ b/solution.py
@@ -362,7 +362,7 @@
     aggregated = pl.pallas_call(
         functools.partial(kernel, slots, pairs, row_tiles, block),
         name="graph_layer",
-        out_shape=jax.ShapeDtypeStruct((block, size, width), jnp.bfloat16),
+        out_shape=pltpu.VMEM((block, size, width), jnp.bfloat16),
         in_specs=[vmem, vmem, vmem, hbm, hbm],
         out_specs=vmem,
         scratch_shapes=[
@@ -378,7 +378,7 @@
             dma((3,)), dma, dma((8,)), dma((CHUNKS,)), dma((CHUNKS, 14)), dma((CHUNKS,)), dma((CHUNKS,)), dma((CHUNKS,)), dma((CHUNKS, 14)),
         ],
         compiler_params=pltpu.CompilerParams(
-            collective_id=0, has_side_effects=True, vmem_limit_bytes=67043328
+            collective_id=0, has_side_effects=True, vmem_limit_bytes=65500000
         ),
     )(
         tile_rows[0], tile_cols[0], valid[0],

time: 109 us -> 107 us (0.982)
  matrix products: 2.72 us -> 1.4 us
    dot_general x1, matrix products: 2.72 us -> 1.4 us  [on_device(): jnp.dot(aggregated.reshape(sub_rows, width), weight, preferred_element_ty...]
where the time goes in v5:
time: 107 us; the launch traced here: 106 us
  Pallas kernels  105 us (98%)
  matrix products  1.4 us (1%)
    pallas_call x1, Pallas kernels, on_device(): pl.pallas_call(functools.partial(kernel, slots, pairs, row_tiles, block),...  105 us

profile of v5, /device:TPU:1, one launch (start us, length us, event | category | flops | bytes accessed | tf_op | source)
XLA Modules:
  0.0 106.4 jit_solution(4497957994394173465)
XLA Ops:
  0.0 0.0 copy-start
  0.0 0.0 copy-start.1
  0.0 105.0 %graph_layer.1 = bf16[16,128,256]{2,1,0:T(8,128)(2,1)S(1)} custom-call(s32[1,768]{1,0:T(1,128)} %bitcast.11, s32[1,768]{1,0:T(1,128)} %bitcast.12, s32[1,768]{1,0:T(1,128)} %bitcast.13, bf16[16,128,256]{2,1,0:T(8,128)(2,1)} %bitcast.10, bf16[768,128,128]{2,1,0:T(8,128)(2,1)} %bitcast.9), custom_call_target="tpu_custom_call" | custom-call | tf_op jit(solution)/shard_map/graph_layer/pallas_call | solution.py:362
  105.0 0.0 copy-done
  105.0 0.0 copy-done.1
  105.0 1.4 %fusion.1 = bf16[2048,256]{1,0:T(8,128)(2,1)} fusion(bf16[2048,256]{1,0:T(8,128)(2,1)S(1)} %bitcast.8, bf16[256,256]{1,0:T(8,128)(2,1)S(1)} %copy-done, f32[256]{0:T(256)S(1)} %copy-done.1), kind=kOutput, calls=%fused_computation.2 | convolution fusion | flops 270008320 | bytes 2229248 | tf_op jit(solution)/shard_map/dot_general | solution.py:387
Async XLA Ops:
  0.0 105.0 %copy-start = (bf16[256,256]{1,0:T(8,128)(2,1)S(1)}, bf16[256,256]{1,0:T(8,128)(2,1)}, u32[]{:S(2)}) copy-start(bf16[256,256]{1,0:T(8,128)(2,1)} %param.12) | copy-start | bytes 393220
  0.0 105.0 %copy-start.1 = (f32[256]{0:T(256)S(1)}, f32[256]{0:T(256)}, u32[]{:S(2)}) copy-start(f32[256]{0:T(256)} %param.13) | copy-start | bytes 3076
